TPU v7x, 32 devices: a whole 2x2x4 slice. The times are simulated.
32 devices in a mesh: morton: 8 (over y, x, core), group: 4 (over z).
Axes of the slice: x: 2, y: 2, z: 4, core: 2. Of those that a mesh axis runs over, the one named last changes fastest.
Arguments:
- state: float32 [4, 64, 5, 512], P('group', 'morton'), may hold values from -12 to 110, as said below
- patch_count: int32 [8], P('morton'), may hold values from 1 to 8, as said below
- neighbour_table: int32 [8, 8, 4], P('morton'), may hold values from -1 to 63, as said below
- send_table: int32 [8, 8, 5], P('morton'), may hold values from -1 to 31, as said below
- ghost_table: int32 [8, 8, 4], P('morton'), may hold values from -1 to 39, as said below
Outputs:
- updated: float32 [4, 64, 5, 512], P('group', 'morton')
Inputs may be any that keep to these rules, and one draw needn't show every extreme that they name: `state`: density lies in [0.5, 2] and the pressure implied by the five variables in [0.1, 0.4] in every live cell. `patch_count`: range i holds slab-order positions starting[i] to starting[i+1] - 1, where starting[i] = i * 4 + j[i] with |j[i]| <= 2 and j[0] = j[8] = 0; some range holds 8. `neighbour_table`: global slot = range * 8 + local slot; slab positions form rows of 4; faces 0 and 1 meet positions -4 and +4, faces 2 and 3 the neighbours in the row; empty slots and domain walls give -1. `send_table`: entry [i, j, t] is -1 or local slot * 4 + face of a patch of range i whose face goes to slot t of the message from i to j; messages of some pair use all 5 slots. `ghost_table`: -1 for faces whose neighbour is held by the same range or absent; else i * 5 + t for the face sent by range i in slot t, and i lies within 2 of the receiving range.
All inputs are finite; a program needn't handle non-finite values.
Results may differ from a plain program's by a relative error of at most 0.00002.
Values sent between devices are 32-bit elements; how exact they have to be, the bound alone decides.
A program may use at most 64 MiB of HBM per device.

v0:
```python
import jax
import jax.numpy as jnp
from jax import lax
from jax.sharding import PartitionSpec as P

EDGE = 8
VARS = 5


GAMMA = 1.4
COURANT = 0.8


def shifted(value, axis, steps):
    count = lax.axis_size(axis)
    leading, last = (max(0, -steps), min(count, count - steps))
    return lax.ppermute(value, axis, [(source, source + steps) for source in range(leading, last)])


def padded(shard, sides, width):
    for axis, dim in sides:
        peers, length = (lax.axis_size(axis), shard.shape[dim])
        up = [(i, (i + 1) % peers) for i in range(peers - 1)]
        down = [(j, i) for i, j in up]
        last = lax.slice_in_dim(shard, length - width, length, axis=dim)
        leading = lax.slice_in_dim(shard, 0, width, axis=dim)
        before = lax.ppermute(last, axis, up)
        after = lax.ppermute(leading, axis, down)
        shard = jnp.concatenate([before, shard, after], axis=dim)
    return shard


def face_layer(blocks, direction):
    if direction == 0:
        return blocks[..., 0, :, :]
    if direction == 1:
        return blocks[..., -1, :, :]
    if direction == 2:
        return blocks[..., :, 0, :]
    if direction == 3:
        return blocks[..., :, -1, :]
    if direction == 4:
        return blocks[..., :, :, 0]
    return blocks[..., :, :, -1]


def primitives(cells_flat):
    density = cells_flat[..., 0, :]
    momenta = cells_flat[..., 1:4, :]
    energy = cells_flat[..., 4, :]
    velocity = momenta / density[..., None, :]
    pressure = (GAMMA - 1.0) * (energy - 0.5 * jnp.sum(momenta * velocity, axis=-2))
    sound = jnp.sqrt(GAMMA * pressure / density)
    return (density, momenta, energy, velocity, pressure, sound)


def wave_bound(cells_flat):
    density, momenta, energy, velocity, pressure, sound = primitives(cells_flat)
    return jnp.sum(jnp.abs(velocity), axis=-2) + 3.0 * sound


def euler_flux(cells_flat, normal_axis):
    density, momenta, energy, velocity, pressure, sound = primitives(cells_flat)
    normal = velocity[..., normal_axis, :]
    parts = [momenta[..., normal_axis, :]]
    for compon in range(3):
        term = momenta[..., compon, :] * normal
        if compon == normal_axis:
            term = term + pressure
        parts.append(term)
    parts.append((energy + pressure) * normal)
    return (jnp.stack(parts, axis=-2), jnp.abs(normal) + sound)


def rusanov(left, right, normal_axis):
    flux_left, speed_left = euler_flux(left, normal_axis)
    flux_right, speed_right = euler_flux(right, normal_axis)
    speed = jnp.maximum(speed_left, speed_right)
    return 0.5 * (flux_left + flux_right) - 0.5 * speed[..., None, :] * (right - left)


def spread_face(face, normal_axis):
    if normal_axis == 0:
        widened = face[..., None, :, :]
    elif normal_axis == 1:
        widened = face[..., :, None, :]
    else:
        widened = face[..., :, :, None]
    full_shape = face.shape[:-2] + (EDGE, EDGE, EDGE)
    return jnp.broadcast_to(widened, full_shape).reshape(face.shape[:-2] + (EDGE * EDGE * EDGE,))


def divergence_flat(cells_flat, ghosts):
    cell_ids = jnp.arange(EDGE * EDGE * EDGE, dtype=jnp.int32)
    total = None
    for normal_axis in range(3):
        stride = EDGE ** (2 - normal_axis)
        position = cell_ids // stride % EDGE
        lower_full = spread_face(ghosts[2 * normal_axis], normal_axis)
        upper_full = spread_face(ghosts[2 * normal_axis + 1], normal_axis)
        left = jnp.where(position == 0, lower_full, jnp.roll(cells_flat, stride, axis=-1))
        right = jnp.where(position == EDGE - 1, upper_full, jnp.roll(cells_flat, -stride, axis=-1))
        term = rusanov(cells_flat, right, normal_axis) - rusanov(left, cells_flat, normal_axis)
        total = term if total is None else total + term
    return total


def per_device(state, patch_count, neighbour_table, send_table, ghost_table):
    slots = state.shape[1]
    message = send_table.shape[2]
    ranges = lax.axis_size("morton")
    myself = lax.axis_index("morton")
    cells_flat = state[0]
    blocks = cells_flat.reshape(slots, VARS, EDGE, EDGE, EDGE)
    valid = jnp.arange(slots, dtype=jnp.int32) < patch_count[0]
    local_top = jnp.max(jnp.where(valid[:, None], wave_bound(cells_flat), jnp.float32(0.0)))
    top_speed = lax.pmax(local_top, ("morton", "group"))
    step_size = COURANT / top_speed
    layers = jnp.stack([face_layer(blocks, direction) for direction in range(4)], axis=1)
    width = VARS * EDGE * EDGE
    own_faces = layers.reshape(slots * 4, width)

    def gather_faces(table_entries):
        picked = jnp.take(own_faces, jnp.maximum(table_entries, 0), axis=0)
        return jnp.where((table_entries >= 0)[..., None], picked, jnp.float32(0.0))

    def outgoing(offset):
        wanted = jnp.clip(myself + offset, 0, ranges - 1)
        target_entries = lax.dynamic_index_in_dim(send_table[0], wanted, 0, keepdims=False)
        return gather_faces(target_entries)

    ghost_index = ghost_table[0].reshape(slots * 4)
    stacked = [jnp.zeros((message, width), jnp.float32) for number in range(5)]
    for sign in (-1, 1):
        pair = jnp.stack([outgoing(sign), outgoing(2 * sign)])
        arrived = shifted(pair, "morton", sign)
        stacked[2 - sign] = arrived[0]
        onward = shifted(arrived[1], "morton", sign)
        stacked[2 - 2 * sign] = onward
    received = jnp.stack(stacked).reshape(-1, width)
    lookup = jnp.where(
        ghost_index >= 0,
        (ghost_index // message - myself + 2) * message + ghost_index % message,
        -1,
    )
    remote_faces = jnp.take(received, jnp.clip(lookup, 0, 5 * message - 1), axis=0)
    neighbours = neighbour_table[0].reshape(slots * 4)
    owners = neighbours // slots
    is_local = (neighbours >= 0) & (owners == myself)
    positions = jnp.arange(slots * 4, dtype=jnp.int32)
    directions = positions % 4
    opposite = directions + 1 - 2 * (directions % 2)
    local_index = jnp.where(is_local, neighbours % slots * 4 + opposite, positions)
    local_faces = jnp.take(own_faces, local_index, axis=0)
    ghost_faces = jnp.where((ghost_index >= 0)[:, None], remote_faces, local_faces)
    lateral = ghost_faces.reshape(slots, 4, VARS, EDGE, EDGE)
    vertical = jnp.stack([face_layer(blocks, 4), face_layer(blocks, 5)])
    extended = padded(vertical, (("group", 0),), 1)
    slab_index = lax.axis_index("group")
    lower = jnp.where(slab_index == 0, vertical[0], extended[0])
    upper = jnp.where(slab_index == lax.axis_size("group") - 1, vertical[1], extended[3])
    ghosts = [lateral[:, direction] for direction in range(4)] + [lower, upper]
    change = divergence_flat(cells_flat, ghosts)
    result = jnp.where(valid[:, None, None], cells_flat - step_size * change, jnp.float32(0.0))
    return result.reshape(1, slots, VARS, EDGE * EDGE * EDGE)


def solution(mesh):
    placed = (
        P("group", "morton", None, None),
        P("morton"),
        P("morton", None, None),
        P("morton", None, None),
        P("morton", None, None),
    )
    return jax.shard_map(
        per_device,
        mesh=mesh,
        in_specs=placed,
        out_specs=P("group", "morton", None, None),
        check_vma=False,
    )
```

profile of v0, /device:TPU:5, one launch (start us, length us, event | category | flops | bytes accessed | tf_op | source)
XLA Modules:
  0.0 141.3 jit_solution(16489286784947655390)
XLA Ops:
  0.0 1.3 maximum_reduce_fusion.1
  1.3 1.4 compare_reduce_fusion.1
  2.7 1.6 %reshape_squeeze.9 = f32[8,5,8,8,8]{4,3,2,0,1:T(8,128)S(1)} reshape(f32[1,8,5,512]{3,1,2,0:T(8,128)} %param.7) | data formatting | bytes 163840 | tf_op jit(solution)/shard_map/reshape;squeeze | solution.py:114
  6.9 3.7 %collective-permute-start = (f32[2,5,320]{2,1,0:T(8,128)}, f32[2,5,320]{2,1,0:T(8,128)}, u32[]{:S(2)}, u32[]{:S(2)}) collective-permute-start(f32[2,5,320]{2,1,0:T(8,128)} %pad_maximum_fusion.1), channel_id=1, source_target_pairs={{0,4},{4,8},{8,12},{12,16},{16,20},{20,24},{24,28},{1,5},{5,9},{9,... | collective-permute-start | bytes 38408 | tf_op jit(solution)/shard_map/ppermute | solution.py:17
  12.5 1.9 %collective-permute-start.2 = (f32[2,5,320]{2,1,0:T(8,128)}, f32[2,5,320]{2,1,0:T(8,128)}, u32[]{:S(2)}, u32[]{:S(2)}) collective-permute-start(f32[2,5,320]{2,1,0:T(8,128)} %pad_maximum_fusion.2), channel_id=1, source_target_pairs={{4,0},{8,4},{12,8},{16,12},{20,16},{24,20},{28,24},{5,1},{9,5},{13... | collective-permute-start | bytes 38408 | tf_op jit(solution)/shard_map/ppermute | solution.py:17
  14.4 1.6 %fusion.89 = (f32[8,5,8,8,1]{4,3,2,0,1:T(8,128)S(1)}, f32[8,5,8,8,1]{4,3,2,0,1:T(8,128)}) fusion(f32[8,5,8,8,8]{4,3,2,0,1:T(8,128)S(1)} %reshape_squeeze.9), kind=kLoop, calls=%fused_computation.321 | loop fusion | bytes 40960 | tf_op jit(solution)/shard_map/slice | solution.py:44
  16.0 3.9 %copy.87 = f32[8,5,8,8,1]{3,2,1,0,4:T(8,128)} copy(f32[8,5,8,8,1]{4,3,2,0,1:T(8,128)} %get-tuple-element.38) | data formatting | bytes 20480 | tf_op jit(solution)/shard_map/slice | solution.py:43
  19.9 1.3 collective-permute-start.4
  21.2 2.6 %copy.92 = f32[8,5,8,8,1]{3,2,1,0,4:T(8,128)} copy(f32[8,5,8,8,1]{4,3,2,0,1:T(8,128)S(1)} %get-tuple-element.37) | data formatting | bytes 20480 | tf_op jit(solution)/shard_map/slice | solution.py:44
  23.8 4.0 %collective-permute-start.5 = (f32[1,8,5,8,8]{4,3,2,1,0:T(8,128)}, f32[1,8,5,8,8]{4,3,2,1,0:T(8,128)S(1)}, u32[]{:S(2)}, u32[]{:S(2)}) collective-permute-start(f32[1,8,5,8,8]{4,3,2,1,0:T(8,128)} %bitcast.97), channel_id=1, source_target_pairs={{0,1},{1,2},{2,3},{4,5},{5,6},{6,7},{8,9},{9,10},{10,11},{12,13},{... | collective-permute-start | bytes 30728 | tf_op jit(solution)/shard_map/ppermute | solution.py:27
  29.7 0.7 fusion.96
  30.3 0.7 fusion.94
  31.0 0.7 fusion.91
  31.7 0.8 fusion.95
  32.5 0.8 fusion.93
  33.3 0.8 fusion.92
  36.2 0.7 fusion.44
  36.9 41.9 %pmax.7 = f32[]{:T(128)} all-reduce(f32[]{:T(128)} %fusion.44), channel_id=1, replica_groups=mesh['morton'=8,'group'=4] {'morton','group'}, use_global_device_ids=true, to_apply=%region_3.4 | all-reduce | flops 1 | bytes 8 | tf_op jit(solution)/shard_map/pmax | solution.py:117
  78.8 0.7 copy.71
  82.8 2.8 %copy.93 = f32[8,5,8,8,1]{4,3,2,0,1:T(8,128)S(1)} copy(f32[8,5,8,8,1]{3,2,1,0,4:T(8,128)} %bitcast.407) | data formatting | bytes 20480 | tf_op jit(solution)/shard_map/squeeze | solution.py:160
  85.7 3.9 %copy.88 = f32[8,5,8,8,1]{4,3,2,0,1:T(8,128)} copy(f32[8,5,8,8,1]{3,2,1,0,4:T(8,128)} %bitcast.84) | data formatting | bytes 20480 | tf_op jit(solution)/shard_map/squeeze | solution.py:161
  89.6 3.3 %broadcast_select_fusion = (f32[8,5,8,8,1]{4,3,2,0,1:T(8,128)}, f32[8,5,8,8,1]{4,3,2,0,1:T(8,128)}) fusion(f32[8,5,8,8,1]{4,3,2,0,1:T(8,128)S(1)} %copy.93, pred[]{:T(512)S(6)} %eq.70, f32[8,5,8,8,8]{4,3,2,0,1:T(8,128)S(1)} %reshape_squeeze.9, f32[8,5,8,8,1]{4,3,2,0,1:T(8,128)} %copy.88, pred[]{:T(512)S(6)} %eq.68), kind=kLoop, calls=%fused_computation.8 | loop fusion | flops 5120 | bytes 61442 | tf_op jit(solution)/shard_map/jit(_where)/select_n | solution.py:160
  92.9 4.0 %copy.99 = f32[8,5,8,8,1]{3,2,0,1,4:T(8,128)} copy(f32[8,5,8,8,1]{4,3,2,0,1:T(8,128)} %get-tuple-element.35) | data formatting | bytes 20480 | tf_op jit(solution)/shard_map/broadcast_in_dim | solution.py:90
  96.9 1.9 %copy.98 = f32[8,5,8,8,1]{3,2,0,1,4:T(8,128)S(1)} copy(f32[8,5,8,8,1]{4,3,2,0,1:T(8,128)S(1)} %copy-done.1) | data formatting | bytes 20480 | tf_op jit(solution)/shard_map/broadcast_in_dim | solution.py:90
  99.3 1.3 reshape.1559
  100.6 1.3 broadcast_in_dim.213
  101.9 1.3 reshape.1561
  103.2 1.1 maximum_select_fusion.8
  109.2 0.7 slice_bitcast_fusion.14
  109.9 4.4 %collective-permute-start.1 = (f32[5,320]{1,0:T(8,128)S(1)}, f32[5,320]{1,0:T(8,128)S(1)}, u32[]{:S(2)}, u32[]{:S(2)}) collective-permute-start(f32[5,320]{1,0:T(8,128)S(1)} %slice_bitcast_fusion.14), channel_id=1, source_target_pairs={{0,4},{4,8},{8,12},{12,16},{16,20},{20,24},{24,28},{1,5},{5,9},{9,... | collective-permute-start | bytes 19208 | tf_op jit(solution)/shard_map/ppermute | solution.py:17
  115.8 1.3 constant_dynamic-update-slice_fusion.8
  117.7 1.3 slice_bitcast_fusion.13
  119.0 4.2 %collective-permute-start.3 = (f32[5,320]{1,0:T(8,128)}, f32[5,320]{1,0:T(8,128)}, u32[]{:S(2)}, u32[]{:S(2)}) collective-permute-start(f32[5,320]{1,0:T(8,128)} %get-tuple-element.87), channel_id=1, source_target_pairs={{4,0},{8,4},{12,8},{16,12},{20,16},{24,20},{28,24},{5,1},{9,5},{13... | collective-permute-start | bytes 19208 | tf_op jit(solution)/shard_map/ppermute | solution.py:17
  123.9 1.3 reshape.1560
  125.2 1.3 reshape.1562
  126.5 1.3 constant_dynamic-update-slice_fusion.5
  127.8 0.8 reshape.1550
  128.6 0.7 gather_fusion
  130.0 0.7 reshape.1552
  130.7 0.7 reshape.1551
  131.6 0.7 reshape.1554
  132.3 0.7 reshape.1553
  133.8 0.7 reshape.1556
  134.5 0.7 reshape.1555
  136.1 0.7 reshape.1558
  136.8 0.7 reshape.1557
  138.4 0.8 multiply_bitcast_fusion.3
  139.5 1.8 %fusion.8 = f32[1,8,5,512]{3,1,2,0:T(8,128)} fusion(f32[1,8,5,512]{3,1,2,0:T(8,128)S(1)} %copy-done, f32[1,8,5,512]{3,1,2,0:T(8,128)S(1)} %reshape.1552, f32[1,8,5,64]{3,1,2,0:T(8,128)S(1)} %copy-done.26, f32[1,8,5,448]{3,1,2,0:T(8,128)S(1)} %copy-done.8, f32[1,8,5,512]{3,1,2,0:T(8,128)S(1)} %reshape.1554, f32[1,8,5,448]{3,1,2,0:T(8,128)S(1)} %copy-done.9, ...), kind=kLoop, calls=%fused_computation.76 | loop fusion | flops 1024000 | bytes 1985548 | tf_op jit(solution)/shard_map/jit(_where)/select_n | solution.py:164
  (230 shorter events, 21.6 us)
Async XLA Ops:
  6.9 102.3 %collective-permute-start = (f32[2,5,320]{2,1,0:T(8,128)}, f32[2,5,320]{2,1,0:T(8,128)}, u32[]{:S(2)}, u32[]{:S(2)}) collective-permute-start(f32[2,5,320]{2,1,0:T(8,128)} %pad_maximum_fusion.1), channel_id=1, source_target_pairs={{0,4},{4,8},{8,12},{12,16},{16,20},{20,24},{24,28},{1,5},{5,9},{9,... | collective-permute-start | bytes 38408 | tf_op jit(solution)/shard_map/ppermute | solution.py:17
  12.5 105.2 %collective-permute-start.2 = (f32[2,5,320]{2,1,0:T(8,128)}, f32[2,5,320]{2,1,0:T(8,128)}, u32[]{:S(2)}, u32[]{:S(2)}) collective-permute-start(f32[2,5,320]{2,1,0:T(8,128)} %pad_maximum_fusion.2), channel_id=1, source_target_pairs={{4,0},{8,4},{12,8},{16,12},{20,16},{24,20},{28,24},{5,1},{9,5},{13... | collective-permute-start | bytes 38408 | tf_op jit(solution)/shard_map/ppermute | solution.py:17
  16.0 13.0 %copy-start.34 = (s32[1,8,4]{1,2,0:T(4,128)S(1)}, s32[1,8,4]{1,2,0:T(4,128)}, u32[]{:S(2)}) copy-start(s32[1,8,4]{1,2,0:T(4,128)} %param.9) | copy-start | bytes 388
  16.0 13.0 %copy-start.35 = (s32[1,8,4]{1,2,0:T(4,128)S(1)}, s32[1,8,4]{1,2,0:T(4,128)}, u32[]{:S(2)}) copy-start(s32[1,8,4]{1,2,0:T(4,128)} %param.11) | copy-start | bytes 388
  16.0 13.1 %copy-start = (f32[1,8,5,512]{3,1,2,0:T(8,128)S(1)}, f32[1,8,5,512]{3,1,2,0:T(8,128)}, u32[]{:S(2)}) copy-start(f32[1,8,5,512]{3,1,2,0:T(8,128)} %param.7) | copy-start | bytes 245764
  19.9 65.8 %collective-permute-start.4 = (f32[1,8,5,8,8]{4,3,2,1,0:T(8,128)}, f32[1,8,5,8,8]{4,3,2,1,0:T(8,128)}, u32[]{:S(2)}, u32[]{:S(2)}) collective-permute-start(f32[1,8,5,8,8]{4,3,2,1,0:T(8,128)} %bitcast.83), channel_id=1, source_target_pairs={{1,0},{2,1},{3,2},{5,4},{6,5},{7,6},{9,8},{10,9},{11,10},{13,12},{... | collective-permute-start | bytes 30728 | tf_op jit(solution)/shard_map/ppermute | solution.py:28
  23.8 58.4 %collective-permute-start.5 = (f32[1,8,5,8,8]{4,3,2,1,0:T(8,128)}, f32[1,8,5,8,8]{4,3,2,1,0:T(8,128)S(1)}, u32[]{:S(2)}, u32[]{:S(2)}) collective-permute-start(f32[1,8,5,8,8]{4,3,2,1,0:T(8,128)} %bitcast.97), channel_id=1, source_target_pairs={{0,1},{1,2},{2,3},{4,5},{5,6},{6,7},{8,9},{9,10},{10,11},{12,13},{... | collective-permute-start | bytes 30728 | tf_op jit(solution)/shard_map/ppermute | solution.py:27
  27.8 75.4 %copy-start.45 = (pred[512]{0:T(512)(128)(4,1)}, pred[512]{0:T(512)(128)(4,1)S(1)}, u32[]{:S(2)}) copy-start(pred[512]{0:T(512)(128)(4,1)S(1)} %fusion.52) | copy-start | bytes 1540
  34.8 50.9 %copy-start.43 = (pred[8]{0:T(512)(128)(4,1)}, pred[8]{0:T(512)(128)(4,1)S(1)}, u32[]{:S(2)}) copy-start(pred[8]{0:T(512)(128)(4,1)S(1)} %iota_compare_fusion) | copy-start | bytes 28
  36.2 43.9 %copy-start.19 = (f32[8,512]{1,0:T(8,128)}, f32[8,512]{1,0:T(8,128)S(1)}, u32[]{:S(2)}) copy-start(f32[8,512]{1,0:T(8,128)S(1)} %get-tuple-element.7) | copy-start | bytes 49156
  36.9 66.3 %copy-start.47 = (pred[512]{0:T(512)(128)(4,1)}, pred[512]{0:T(512)(128)(4,1)S(1)}, u32[]{:S(2)}) copy-start(pred[512]{0:T(512)(128)(4,1)S(1)} %fusion.51) | copy-start | bytes 1540
  92.9 4.0 %copy-start.1 = (f32[8,5,8,8,1]{4,3,2,0,1:T(8,128)S(1)}, f32[8,5,8,8,1]{4,3,2,0,1:T(8,128)}, u32[]{:S(2)}) copy-start(f32[8,5,8,8,1]{4,3,2,0,1:T(8,128)} %get-tuple-element.36) | copy-start | bytes 30724
  104.3 19.0 %copy-start.2 = (f32[8,5,512]{2,0,1:T(8,128)}, f32[8,5,512]{2,0,1:T(8,128)S(1)}, u32[]{:S(2)}) copy-start(f32[8,5,512]{2,0,1:T(8,128)S(1)} %get-tuple-element.101) | copy-start | bytes 245764
  105.6 17.7 %copy-start.3 = (f32[8,3,512]{2,0,1:T(8,128)}, f32[8,3,512]{2,0,1:T(8,128)S(1)}, u32[]{:S(2)}) copy-start(f32[8,3,512]{2,0,1:T(8,128)S(1)} %get-tuple-element.31) | copy-start | bytes 147460
  105.6 17.7 %copy-start.16 = (f32[8,512]{1,0:T(8,128)}, f32[8,512]{1,0:T(8,128)S(1)}, u32[]{:S(2)}) copy-start(f32[8,512]{1,0:T(8,128)S(1)} %get-tuple-element.30) | copy-start | bytes 49156
  109.9 5.3 %collective-permute-start.1 = (f32[5,320]{1,0:T(8,128)S(1)}, f32[5,320]{1,0:T(8,128)S(1)}, u32[]{:S(2)}, u32[]{:S(2)}) collective-permute-start(f32[5,320]{1,0:T(8,128)S(1)} %slice_bitcast_fusion.14), channel_id=1, source_target_pairs={{0,4},{4,8},{8,12},{12,16},{16,20},{20,24},{24,28},{1,5},{5,9},{9,... | collective-permute-start | bytes 19208 | tf_op jit(solution)/shard_map/ppermute | solution.py:17
  119.0 7.4 %collective-permute-start.3 = (f32[5,320]{1,0:T(8,128)}, f32[5,320]{1,0:T(8,128)}, u32[]{:S(2)}, u32[]{:S(2)}) collective-permute-start(f32[5,320]{1,0:T(8,128)} %get-tuple-element.87), channel_id=1, source_target_pairs={{4,0},{8,4},{12,8},{16,12},{20,16},{24,20},{28,24},{5,1},{9,5},{13... | collective-permute-start | bytes 19208 | tf_op jit(solution)/shard_map/ppermute | solution.py:17
  125.2 4.4 %copy-start.49 = (pred[8,4]{1,0:T(8,128)(4,1)S(1)}, pred[8,4]{1,0:T(8,128)(4,1)}, u32[]{:S(2)}) copy-start(pred[8,4]{1,0:T(8,128)(4,1)} %copy.71) | copy-start | bytes 100
  125.2 4.4 %copy-start.50 = (pred[8,4]{1,0:T(8,128)(4,1)S(1)}, pred[8,4]{1,0:T(8,128)(4,1)}, u32[]{:S(2)}) copy-start(pred[8,4]{1,0:T(8,128)(4,1)} %copy.81) | copy-start | bytes 100
  125.2 4.4 %copy-start.51 = (pred[8,4]{1,0:T(8,128)(4,1)S(1)}, pred[8,4]{1,0:T(8,128)(4,1)}, u32[]{:S(2)}) copy-start(pred[8,4]{1,0:T(8,128)(4,1)} %copy.70) | copy-start | bytes 100
  130.0 1.4 copy-start.15
  131.6 1.4 copy-start.14
  133.8 1.4 copy-start.13
  133.8 1.3 copy-start.29
  136.1 1.4 copy-start.12
  136.1 1.4 copy-start.28
  136.1 1.4 copy-start.36
  136.1 1.5 %copy-start.20 = (f32[8,512]{1,0:T(8,128)S(1)}, f32[8,512]{1,0:T(8,128)}, u32[]{:S(2)}) copy-start(f32[8,512]{1,0:T(8,128)} %copy-done.19) | copy-start | bytes 49156
  137.7 1.6 %copy-start.4 = (f32[1,8,5,511]{3,1,2,0:T(8,128)S(1)}, f32[1,8,5,511]{3,1,2,0:T(8,128)}, u32[]{:S(2)}) copy-start(f32[1,8,5,511]{3,1,2,0:T(8,128)} %get-tuple-element.75) | copy-start | bytes 245284
  137.7 1.6 %copy-start.5 = (f32[1,8,5,511]{3,1,2,0:T(8,128)S(1)}, f32[1,8,5,511]{3,1,2,0:T(8,128)}, u32[]{:S(2)}) copy-start(f32[1,8,5,511]{3,1,2,0:T(8,128)} %get-tuple-element.76) | copy-start | bytes 245284
  137.7 1.6 %copy-start.6 = (f32[1,8,5,504]{3,1,2,0:T(8,128)S(1)}, f32[1,8,5,504]{3,1,2,0:T(8,128)}, u32[]{:S(2)}) copy-start(f32[1,8,5,504]{3,1,2,0:T(8,128)} %get-tuple-element.67) | copy-start | bytes 241924
  137.7 1.6 %copy-start.7 = (f32[1,8,5,504]{3,1,2,0:T(8,128)S(1)}, f32[1,8,5,504]{3,1,2,0:T(8,128)}, u32[]{:S(2)}) copy-start(f32[1,8,5,504]{3,1,2,0:T(8,128)} %get-tuple-element.68) | copy-start | bytes 241924
  137.7 1.6 %copy-start.8 = (f32[1,8,5,448]{3,1,2,0:T(8,128)S(1)}, f32[1,8,5,448]{3,1,2,0:T(8,128)}, u32[]{:S(2)}) copy-start(f32[1,8,5,448]{3,1,2,0:T(8,128)} %get-tuple-element.63) | copy-start | bytes 215044
  137.7 1.6 %copy-start.9 = (f32[1,8,5,448]{3,1,2,0:T(8,128)S(1)}, f32[1,8,5,448]{3,1,2,0:T(8,128)}, u32[]{:S(2)}) copy-start(f32[1,8,5,448]{3,1,2,0:T(8,128)} %get-tuple-element.64) | copy-start | bytes 215044
  137.7 1.6 %copy-start.10 = (f32[1,8,5,512]{3,1,2,0:T(8,128)S(1)}, f32[1,8,5,512]{3,1,2,0:T(8,128)}, u32[]{:S(2)}) copy-start(f32[1,8,5,512]{3,1,2,0:T(8,128)} %reshape.1560) | copy-start | bytes 245764
  137.7 1.6 %copy-start.11 = (f32[1,8,5,512]{3,1,2,0:T(8,128)S(1)}, f32[1,8,5,512]{3,1,2,0:T(8,128)}, u32[]{:S(2)}) copy-start(f32[1,8,5,512]{3,1,2,0:T(8,128)} %reshape.1562) | copy-start | bytes 245764
  137.8 1.6 %copy-start.22 = (f32[1,8,5,1]{3,1,2,0:T(8,128)S(1)}, f32[1,8,5,1]{3,1,2,0:T(8,128)}, u32[]{:S(2)}) copy-start(f32[1,8,5,1]{3,1,2,0:T(8,128)} %get-tuple-element.79) | copy-start | bytes 484
  137.8 1.6 %copy-start.23 = (f32[1,8,5,1]{3,1,2,0:T(8,128)S(1)}, f32[1,8,5,1]{3,1,2,0:T(8,128)}, u32[]{:S(2)}) copy-start(f32[1,8,5,1]{3,1,2,0:T(8,128)} %get-tuple-element.80) | copy-start | bytes 484
  137.8 1.6 %copy-start.24 = (f32[1,8,5,8]{3,1,2,0:T(8,128)S(1)}, f32[1,8,5,8]{3,1,2,0:T(8,128)}, u32[]{:S(2)}) copy-start(f32[1,8,5,8]{3,1,2,0:T(8,128)} %get-tuple-element.71) | copy-start | bytes 3844
  137.8 1.6 %copy-start.25 = (f32[1,8,5,8]{3,1,2,0:T(8,128)S(1)}, f32[1,8,5,8]{3,1,2,0:T(8,128)}, u32[]{:S(2)}) copy-start(f32[1,8,5,8]{3,1,2,0:T(8,128)} %get-tuple-element.72) | copy-start | bytes 3844
  137.8 1.6 %copy-start.26 = (f32[1,8,5,64]{3,1,2,0:T(8,128)S(1)}, f32[1,8,5,64]{3,1,2,0:T(8,128)}, u32[]{:S(2)}) copy-start(f32[1,8,5,64]{3,1,2,0:T(8,128)} %get-tuple-element.59) | copy-start | bytes 30724
  137.8 1.6 %copy-start.27 = (f32[1,8,5,64]{3,1,2,0:T(8,128)S(1)}, f32[1,8,5,64]{3,1,2,0:T(8,128)}, u32[]{:S(2)}) copy-start(f32[1,8,5,64]{3,1,2,0:T(8,128)} %get-tuple-element.60) | copy-start | bytes 30724
  137.8 1.6 %copy-start.38 = (pred[512]{0:T(512)(128)(4,1)S(1)}, pred[512]{0:T(512)(128)(4,1)}, u32[]{:S(2)}) copy-start(pred[512]{0:T(512)(128)(4,1)} %get-tuple-element.105) | copy-start | bytes 1540
  137.8 1.6 %copy-start.40 = (pred[512]{0:T(512)(128)(4,1)S(1)}, pred[512]{0:T(512)(128)(4,1)}, u32[]{:S(2)}) copy-start(pred[512]{0:T(512)(128)(4,1)} %get-tuple-element.102) | copy-start | bytes 1540
  137.8 1.6 %copy-start.42 = (pred[512]{0:T(512)(128)(4,1)S(1)}, pred[512]{0:T(512)(128)(4,1)}, u32[]{:S(2)}) copy-start(pred[512]{0:T(512)(128)(4,1)} %get-tuple-element.103) | copy-start | bytes 1540
  137.8 1.6 %copy-start.44 = (pred[8]{0:T(512)(128)(4,1)S(1)}, pred[8]{0:T(512)(128)(4,1)}, u32[]{:S(2)}) copy-start(pred[8]{0:T(512)(128)(4,1)} %copy-done.43) | copy-start | bytes 28
  137.9 1.6 %copy-start.46 = (pred[512]{0:T(512)(128)(4,1)S(1)}, pred[512]{0:T(512)(128)(4,1)}, u32[]{:S(2)}) copy-start(pred[512]{0:T(512)(128)(4,1)} %copy-done.45) | copy-start | bytes 1540
  137.9 1.6 %copy-start.48 = (pred[512]{0:T(512)(128)(4,1)S(1)}, pred[512]{0:T(512)(128)(4,1)}, u32[]{:S(2)}) copy-start(pred[512]{0:T(512)(128)(4,1)} %copy-done.47) | copy-start | bytes 1540
  (10 other events, 11.0 us)
where the time goes:
time: 142 us; the launch traced here: 141 us
  local copies, waits for them, and re-layouts  57.6 us (41%)
  blocking collectives  41.9 us (30%)
  other arithmetic  19.6 us (14%)
  starting transfers between devices  19.5 us (14%)
  between operations  2.55 us (2%)
    pmax x1, blocking collectives, per_device(): top_speed = lax.pmax(local_top, ('morton', 'group'))  41.9 us
    ppermute x4, starting transfers between devices, shifted(): lax.ppermute(value, axis, [(source, source + steps) for source in range(l...  14.2 us
    reshape x12, local copies, waits for them, and re-layouts, spread_face(): jnp.broadcast_to(widened, full_shape)  10.4 us
    broadcast_in_dim x13, local copies, waits for them, and re-layouts, spread_face(): jnp.broadcast_to(widened, full_shape)  8.24 us
    unnamed x115, local copies, waits for them, and re-layouts  5.42 us
    slice x2, local copies, waits for them, and re-layouts, face_layer(): return blocks[..., :, :, -1]  4.14 us
    ppermute x1, starting transfers between devices, padded(): before = lax.ppermute(last, axis, up)  3.98 us
    slice x1, local copies, waits for them, and re-layouts, face_layer(): return blocks[..., :, :, 0]  3.93 us
  transfers between devices with their start and end apart: 6, of which 1 were waited for; matrix products, arithmetic and copies ran while one was open for 39% of the time, Pallas kernels for 0%

commit v1 on v0

v1 whole, which is shorter than its diff:
```python
import functools

import jax
import jax.numpy as jnp
from jax import lax
from jax.experimental import pallas as pl
from jax.experimental.pallas import tpu as pltpu
from jax.sharding import PartitionSpec as P

EDGE = 8
VARS = 5
LANES = 128
GAMMA = 1.4
COURANT = 0.8
OFFSETS = (-2, -1, 1, 2)


def prims(cells):
    density, mx, my, mz, energy = cells
    inverse = 1.0 / density
    velocity = (mx * inverse, my * inverse, mz * inverse)
    kinetic = mx * velocity[0] + my * velocity[1] + mz * velocity[2]
    pressure = (GAMMA - 1.0) * (energy - 0.5 * kinetic)
    sound = jnp.sqrt(GAMMA * pressure * inverse)
    return velocity, pressure, sound


def flux_along(cells, prim, axis):
    velocity, pressure, sound = prim
    normal = velocity[axis]
    parts = [cells[1 + axis]]
    for compon in range(3):
        term = cells[1 + compon] * normal
        parts.append(term + pressure if compon == axis else term)
    parts.append((cells[4] + pressure) * normal)
    return parts, jnp.abs(normal) + sound


def kernel(ranges, slabs, slots, message, state_hbm, count_hbm, near_hbm, send_hbm, ghost_hbm, out_hbm,
           state, count, near, send, ghost, faces, rolled, outbox, inbox, vertical, above, below,
           ghosts, top_out, top_in, slab_out, slab_in, result,
           load_sem, table_sem, face_send, face_recv, vert_send, vert_recv,
           top_send, top_recv, slab_send, slab_recv, store_sem):
    me = lax.axis_index("morton")
    slab = lax.axis_index("group")
    tiles = state.shape[2] // LANES

    barrier = pltpu.get_barrier_semaphore()
    for step in range(1, slabs):
        pl.semaphore_signal(barrier, inc=1, device_id={"group": lax.rem(slab + step, slabs)},
                            device_id_type=pl.DeviceIdType.MESH)
    for step in range(1, ranges):
        pl.semaphore_signal(barrier, inc=1, device_id={"morton": lax.rem(me + step, ranges)},
                            device_id_type=pl.DeviceIdType.MESH)

    loads = [
        pltpu.make_async_copy(state_hbm, state, load_sem)
    ]
    tables = [
        pltpu.make_async_copy(source, target, table_sem.at[i])
        for i, (source, target) in enumerate(
            ((count_hbm, count), (near_hbm, near), (send_hbm, send), (ghost_hbm, ghost)))
    ]
    for copy in loads + tables:
        copy.start()

    lane = lax.broadcasted_iota(jnp.int32, (slots, LANES), 1)
    low_half = lane < LANES // 2
    pos_x, pos_y, pos_z = lane // 64, lane // 8 % 8, lane % 8
    sub = lax.broadcasted_iota(jnp.int32, (slots, LANES), 0)

    def permuted(value, index):
        return jnp.take_along_axis(value, index, axis=1, mode="promise_in_bounds")

    for copy in loads:
        copy.wait()
    cells = [
        [state[v, :, pl.ds(c * LANES, LANES)] for v in range(VARS)]
        for c in range(tiles)
    ]
    prim = [prims(cells[c]) for c in range(tiles)]
    tables[0].wait()
    valid = sub < count[0]
    top = None
    for velocity, pressure, sound in prim:
        bound = jnp.abs(velocity[0]) + jnp.abs(velocity[1]) + jnp.abs(velocity[2]) + 3.0 * sound
        bound = jnp.where(valid, bound, 0.0)
        top = bound if top is None else jnp.maximum(top, bound)
    top = jnp.max(top, axis=0, keepdims=True)
    top_out[...] = top

    take_y = lane // 8 % 2 * 64 + lane // 64 * 56 + lane % 8
    take_z = lane // 8 % 2 * 64 + lane % 8 * 8 + lane // 64 * 7
    piece = lane % 64 // 16

    def compact(v, index):
        found = permuted(cells[0][v], index)
        for c in range(1, tiles):
            found = jnp.where(piece == c, permuted(cells[c][v], index), found)
        return found

    own = [
        [jnp.where(low_half, cells[0][v], cells[tiles - 1][v]) for v in range(VARS)],
        [compact(v, take_y) for v in range(VARS)],
        [compact(v, take_z) for v in range(VARS)],
    ]
    face_rows = faces.reshape(2 * slots * 8, LANES)
    rolled_rows = rolled.reshape(2 * slots * 8, LANES)
    zero = jnp.zeros((slots, LANES), jnp.float32)
    for p in range(2):
        for v in range(8):
            value = own[p][v] if v < VARS else zero
            face_rows[pl.ds(p * slots * 8 + v, slots, stride=8), :] = value
            rolled_rows[pl.ds(p * slots * 8 + v, slots, stride=8), :] = (
                pltpu.roll(value, 64, 1) if v < VARS else zero)
    for v in range(VARS):
        vertical[v] = own[2][v]

    tables[2].wait()
    tile_low = lax.broadcasted_iota(jnp.int32, (8, LANES), 1) < LANES // 2
    for o, offset in enumerate(OFFSETS):
        target = lax.rem(me + offset + ranges, ranges)
        for t in range(message):
            entry = send[t, 0, target]
            safe = jnp.maximum(entry, 0)
            face = safe % 4
            index = face // 2 * slots + safe // 4
            straight, turned = faces[index], rolled[index]
            picked = jnp.where(tile_low == (face % 2 == 0), straight, turned)
            outbox[o, t] = jnp.where(entry >= 0, picked, 0.0)

    pl.semaphore_wait(barrier, ranges - 1 + slabs - 1)

    def remote(source, target, send_at, recv_at, device):
        copy = pltpu.make_async_remote_copy(
            src_ref=source, dst_ref=target, send_sem=send_at, recv_sem=recv_at,
            device_id=device, device_id_type=pl.DeviceIdType.MESH)
        copy.start()
        return copy

    top_copies = [
        remote(top_out, top_in.at[step - 1], top_send.at[step - 1], top_recv.at[step - 1],
               {"morton": lax.rem(me + step, ranges)})
        for step in range(1, ranges)
    ]
    face_copies = [
        remote(outbox.at[o], inbox.at[len(OFFSETS) - 1 - o], face_send.at[o], face_recv.at[len(OFFSETS) - 1 - o],
               {"morton": lax.rem(me + offset + ranges, ranges)})
        for o, offset in enumerate(OFFSETS)
    ]
    vert_copies = [
        remote(vertical, below, vert_send.at[0], vert_recv.at[0], {"group": lax.rem(slab + 1, slabs)}),
        remote(vertical, above, vert_send.at[1], vert_recv.at[1], {"group": lax.rem(slab + slabs - 1, slabs)}),
    ]

    def shift_up(values, axis):
        if axis == 0:
            turned = [pltpu.roll(value, 64, 1) for value in values]
            return [jnp.where(low_half, turned[max(c - 1, 0)], turned[c]) for c in range(tiles)]
        return [pltpu.roll(value, 8 if axis == 1 else 1, 1) for value in values]

    def shift_down(values, axis):
        if axis == 0:
            turned = [pltpu.roll(value, 64, 1) for value in values]
            return [jnp.where(low_half, turned[c], turned[min(c + 1, tiles - 1)]) for c in range(tiles)]
        return [pltpu.roll(value, LANES - (8 if axis == 1 else 1), 1) for value in values]

    first, last = [], []
    for axis in range(3):
        if axis == 0:
            first.append([low_half if c == 0 else None for c in range(tiles)])
            last.append([~low_half if c == tiles - 1 else None for c in range(tiles)])
        else:
            position = pos_y if axis == 1 else pos_z
            first.append([position == 0] * tiles)
            last.append([position == EDGE - 1] * tiles)

    change = [[None] * VARS for c in range(tiles)]
    for axis in range(3):
        flux = [flux_along(cells[c], prim[c], axis) for c in range(tiles)]
        speed = [flux[c][1] for c in range(tiles)]
        speed_left = shift_up(speed, axis)
        half_speed = [0.5 * jnp.maximum(speed[c], speed_left[c]) for c in range(tiles)]
        for v in range(VARS):
            here = [cells[c][v] for c in range(tiles)]
            here_flux = [flux[c][0][v] for c in range(tiles)]
            left = shift_up(here, axis)
            left_flux = shift_up(here_flux, axis)
            across = [
                0.5 * (left_flux[c] + here_flux[c]) - half_speed[c] * (here[c] - left[c])
                for c in range(tiles)
            ]
            across = [
                across[c] if first[axis][c] is None else jnp.where(first[axis][c], 0.0, across[c])
                for c in range(tiles)
            ]
            upper = shift_down(across, axis)
            for c in range(tiles):
                if last[axis][c] is not None:
                    upper[c] = jnp.where(last[axis][c], 0.0, upper[c])
                term = upper[c] - across[c]
                change[c][v] = term if change[c][v] is None else change[c][v] + term

    own_flux = [flux_along(own[axis], prims(own[axis]), axis) for axis in range(3)]

    for copy in top_copies:
        copy.wait_recv()
    top = top_out[...]
    for step in range(1, ranges):
        top = jnp.maximum(top, top_in[step - 1])
    slab_out[...] = top
    slab_copies = [
        remote(slab_out, slab_in.at[step - 1], slab_send.at[step - 1], slab_recv.at[step - 1],
               {"group": lax.rem(slab + step, slabs)})
        for step in range(1, slabs)
    ]

    tables[1].wait()
    tables[3].wait()
    for copy in face_copies + vert_copies:
        copy.wait_recv()
    for s in range(slots):
        for p in range(2):
            halves = []
            for k in (2 * p, 2 * p + 1):
                arrives = ghost[0, k, s]
                neighbour = near[0, k, s]
                inside = (neighbour >= 0) & (neighbour // slots == me)
                local = jnp.where(inside, neighbour % slots, s)
                here = jnp.where(inside, rolled[p * slots + local], faces[p * slots + s])
                safe = jnp.maximum(arrives, 0)
                distance = safe // message - me
                box = jnp.where(distance < 0, distance + 2, distance + 1)
                box = jnp.clip(box, 0, len(OFFSETS) - 1)
                there = inbox[box, safe % message]
                halves.append(jnp.where(arrives >= 0, there, here))
            ghosts[p * slots + s] = jnp.where(tile_low, halves[0], halves[1])
    ghost_rows = ghosts.reshape(2 * slots * 8, LANES)
    outer = [
        [ghost_rows[pl.ds(p * slots * 8 + v, slots, stride=8), :] for v in range(VARS)]
        for p in range(2)
    ]
    use_own = jnp.where(low_half, (slab == 0).astype(jnp.int32), (slab == slabs - 1).astype(jnp.int32)) > 0
    outer.append([
        jnp.where(use_own, own[2][v], pltpu.roll(jnp.where(low_half, above[v], below[v]), 64, 1))
        for v in range(VARS)
    ])
    sign = jnp.where(low_half, -1.0, 1.0)
    for axis in range(3):
        outer_flux, outer_speed = flux_along(outer[axis], prims(outer[axis]), axis)
        inner_flux, inner_speed = own_flux[axis]
        half_speed = 0.5 * jnp.maximum(outer_speed, inner_speed)
        for v in range(VARS):
            signed = (sign * (0.5 * (outer_flux[v] + inner_flux[v]))
                      - half_speed * (outer[axis][v] - own[axis][v]))
            for c in range(tiles):
                if axis == 0:
                    if c == 0:
                        change[c][v] = change[c][v] + jnp.where(low_half, signed, 0.0)
                    if c == tiles - 1:
                        change[c][v] = change[c][v] + jnp.where(low_half, 0.0, signed)
                else:
                    if axis == 1:
                        index = (2 * c + pos_x) * 8 + pos_z + jnp.where(pos_y >= 4, 64, 0)
                    else:
                        index = (2 * c + pos_x) * 8 + pos_y + jnp.where(pos_z >= 4, 64, 0)
                    edge = first[axis][c] | last[axis][c]
                    change[c][v] = change[c][v] + jnp.where(edge, permuted(signed, index), 0.0)

    for copy in slab_copies:
        copy.wait_recv()
    for step in range(1, slabs):
        top = jnp.maximum(top, slab_in[step - 1])
    step_size = COURANT / jnp.max(top, axis=1, keepdims=True)
    for c in range(tiles):
        for v in range(VARS):
            value = jnp.where(valid, cells[c][v] - step_size * change[c][v], 0.0)
            result[v, :, pl.ds(c * LANES, LANES)] = value
    stores = [pltpu.make_async_copy(result, out_hbm, store_sem)]
    stores[0].start()
    for copy in top_copies + face_copies + vert_copies + slab_copies:
        copy.wait_send()
    for copy in stores:
        copy.wait()


def solution(mesh):
    ranges, slabs = mesh.shape["morton"], mesh.shape["group"]

    def per_device(state, patch_count, neighbour_table, send_table, ghost_table):
        _, slots, variables, count_cells = state.shape
        message = send_table.shape[2]
        tiles = count_cells // LANES
        f32 = jnp.float32
        vmem, smem, dma = pltpu.VMEM, pltpu.SMEM, pltpu.SemaphoreType.DMA
        state = jnp.transpose(state[0], (1, 0, 2))
        neighbour_table = jnp.transpose(neighbour_table, (0, 2, 1))
        send_table = jnp.transpose(send_table, (2, 0, 1))
        ghost_table = jnp.transpose(ghost_table, (0, 2, 1))
        out = pl.pallas_call(
            functools.partial(kernel, ranges, slabs, slots, message),
            out_shape=jax.ShapeDtypeStruct(state.shape, f32),
            in_specs=[pl.BlockSpec(memory_space=pl.ANY)] * 5,
            out_specs=pl.BlockSpec(memory_space=pl.ANY),
            scratch_shapes=[
                vmem(state.shape, f32),
                smem(patch_count.shape, jnp.int32),
                smem(neighbour_table.shape, jnp.int32),
                smem(send_table.shape, jnp.int32),
                smem(ghost_table.shape, jnp.int32),
                vmem((2 * slots, 8, LANES), f32),
                vmem((2 * slots, 8, LANES), f32),
                vmem((len(OFFSETS), message, 8, LANES), f32),
                vmem((len(OFFSETS), message, 8, LANES), f32),
                vmem((VARS, slots, LANES), f32),
                vmem((VARS, slots, LANES), f32),
                vmem((VARS, slots, LANES), f32),
                vmem((2 * slots, 8, LANES), f32),
                vmem((1, LANES), f32),
                vmem((ranges - 1, 1, LANES), f32),
                vmem((1, LANES), f32),
                vmem((slabs - 1, 1, LANES), f32),
                vmem(state.shape, f32),
                dma,
                dma((4,)),
                dma((len(OFFSETS),)),
                dma((len(OFFSETS),)),
                dma((2,)),
                dma((2,)),
                dma((ranges - 1,)),
                dma((ranges - 1,)),
                dma((slabs - 1,)),
                dma((slabs - 1,)),
                dma,
            ],
            compiler_params=pltpu.CompilerParams(collective_id=0, has_side_effects=True),
        )(state, patch_count, neighbour_table, send_table, ghost_table)
        return jnp.transpose(out, (1, 0, 2))[None]

    placed = (
        P("group", "morton", None, None),
        P("morton"),
        P("morton", None, None),
        P("morton", None, None),
        P("morton", None, None),
    )
    return jax.shard_map(
        per_device,
        mesh=mesh,
        in_specs=placed,
        out_specs=P("group", "morton", None, None),
        check_vma=False,
    )
```

time: 142 us -> 15.9 us (0.11)
  the two profiles are of different devices: /device:TPU:5 before, /device:TPU:0 now
where the time goes in v1:
time: 15.9 us; the launch traced here: 15.7 us
  Pallas kernels  13.5 us (85%)
  local copies, waits for them, and re-layouts  1.53 us (10%)
  between operations  0.66 us (4%)
    pallas_call x1, Pallas kernels, per_device(): pl.pallas_call(functools.partial(kernel, ranges, slabs, slots, message),...  13.5 us
    unnamed x1, local copies, waits for them, and re-layouts  1.53 us

profile of v1, /device:TPU:0, one launch (start us, length us, event | category | flops | bytes accessed | tf_op | source)
XLA Modules:
  0.0 15.7 jit_solution(2027941078588850261)
XLA Ops:
  0.7 13.5 %shard_map.55 = f32[5,8,512]{2,1,0:T(8,128)} custom-call(f32[5,8,512]{2,1,0:T(8,128)} %bitcast.10, s32[1]{0:T(128)S(6)} %copy.7.count_hbm, s32[1,4,8]{2,1,0:T(4,128)} %bitcast.12, s32[5,1,8]{2,1,0:T(1,128)} %bitcast.11, s32[1,4,8]{2,1,0:T(4,128)} %bitcast.13), custom_call_target="tpu_custom_call" | custom-call | tf_op jit(solution)/shard_map/pallas_call | solution.py:300
  14.2 1.5 %copy.8 = f32[1,8,5,512]{3,1,2,0:T(8,128)} copy(f32[1,8,5,512]{3,1,2,0:T(8,128)} %bitcast.9) | data formatting | bytes 163840

commit v2 on v1

--- a/solution.py
+++ b/solution.py
@@ -36,11 +36,11 @@
     return parts, jnp.abs(normal) + sound
 
 
-def kernel(ranges, slabs, slots, message, state_hbm, count_hbm, near_hbm, send_hbm, ghost_hbm, out_hbm,
+def kernel(ranges, slabs, slots, message, state_hbm, count_hbm, near_hbm, send_hbm, ghost_hbm, out_ref,
            state, count, near, send, ghost, faces, rolled, outbox, inbox, vertical, above, below,
-           ghosts, top_out, top_in, slab_out, slab_in, result,
+           ghosts, top_out, top_in, slab_out, slab_in,
            load_sem, table_sem, face_send, face_recv, vert_send, vert_recv,
-           top_send, top_recv, slab_send, slab_recv, store_sem):
+           top_send, top_recv, slab_send, slab_recv):
     me = lax.axis_index("morton")
     slab = lax.axis_index("group")
     tiles = state.shape[2] // LANES
@@ -80,7 +80,7 @@
     ]
     prim = [prims(cells[c]) for c in range(tiles)]
     tables[0].wait()
-    valid = sub < count[0]
+    valid = sub < count[0, 0]
     top = None
     for velocity, pressure, sound in prim:
         bound = jnp.abs(velocity[0]) + jnp.abs(velocity[1]) + jnp.abs(velocity[2]) + 3.0 * sound
@@ -275,13 +275,9 @@
     for c in range(tiles):
         for v in range(VARS):
             value = jnp.where(valid, cells[c][v] - step_size * change[c][v], 0.0)
-            result[v, :, pl.ds(c * LANES, LANES)] = value
-    stores = [pltpu.make_async_copy(result, out_hbm, store_sem)]
-    stores[0].start()
+            out_ref[v, :, pl.ds(c * LANES, LANES)] = value
     for copy in top_copies + face_copies + vert_copies + slab_copies:
         copy.wait_send()
-    for copy in stores:
-        copy.wait()
 
 
 def solution(mesh):
@@ -294,14 +290,15 @@
         f32 = jnp.float32
         vmem, smem, dma = pltpu.VMEM, pltpu.SMEM, pltpu.SemaphoreType.DMA
         state = jnp.transpose(state[0], (1, 0, 2))
+        patch_count = patch_count.reshape(1, 1)
         neighbour_table = jnp.transpose(neighbour_table, (0, 2, 1))
         send_table = jnp.transpose(send_table, (2, 0, 1))
         ghost_table = jnp.transpose(ghost_table, (0, 2, 1))
         out = pl.pallas_call(
             functools.partial(kernel, ranges, slabs, slots, message),
-            out_shape=jax.ShapeDtypeStruct(state.shape, f32),
-            in_specs=[pl.BlockSpec(memory_space=pl.ANY)] * 5,
-            out_specs=pl.BlockSpec(memory_space=pl.ANY),
+            out_shape=pltpu.VMEM(state.shape, f32),
+            in_specs=[pl.BlockSpec(memory_space=pltpu.HBM)] * 5,
+            out_specs=pl.BlockSpec(memory_space=pltpu.VMEM),
             scratch_shapes=[
                 vmem(state.shape, f32),
                 smem(patch_count.shape, jnp.int32),
@@ -320,7 +317,6 @@
                 vmem((ranges - 1, 1, LANES), f32),
                 vmem((1, LANES), f32),
                 vmem((slabs - 1, 1, LANES), f32),
-                vmem(state.shape, f32),
                 dma,
                 dma((4,)),
                 dma((len(OFFSETS),)),
@@ -331,7 +327,6 @@
                 dma((ranges - 1,)),
                 dma((slabs - 1,)),
                 dma((slabs - 1,)),
-                dma,
             ],
             compiler_params=pltpu.CompilerParams(collective_id=0, has_side_effects=True),
         )(state, patch_count, neighbour_table, send_table, ghost_table)

time: 15.9 us -> 14.4 us (0.906)
  local copies, waits for them, and re-layouts: 1.53 us -> 0.64 us
  Pallas kernels: 13.5 us -> 12.9 us
    unnamed x1, local copies, waits for them, and re-layouts: 1.53 us -> 0.64 us
    pallas_call x1, Pallas kernels: 13.5 us -> 12.9 us  [per_device(): pl.pallas_call(functools.partial(kernel, ranges, slabs, slots, message),...]
where the time goes in v2:
time: 14.4 us; the launch traced here: 14.2 us
  Pallas kernels  12.9 us (90%)
  between operations  0.66 us (5%)
  local copies, waits for them, and re-layouts  0.64 us (4%)
    pallas_call x1, Pallas kernels, per_device(): pl.pallas_call(functools.partial(kernel, ranges, slabs, slots, message),...  12.9 us
    unnamed x1, local copies, waits for them, and re-layouts  0.64 us

profile of v2, /device:TPU:0, one launch (start us, length us, event | category | flops | bytes accessed | tf_op | source)
XLA Modules:
  0.0 14.2 jit_solution(15862606220819799700)
XLA Ops:
  0.7 12.9 %shard_map.55 = f32[5,8,512]{2,1,0:T(8,128)S(1)} custom-call(f32[5,8,512]{2,1,0:T(8,128)} %bitcast.12, s32[1,1]{1,0:T(1,128)} %bitcast.10.count_hbm, s32[1,4,8]{2,1,0:T(4,128)} %bitcast.14, s32[5,1,8]{2,1,0:T(1,128)} %bitcast.13, s32[1,4,8]{2,1,0:T(4,128)} %bitcast.15), custom_call_target="tpu_custom_call" | custom-call | tf_op jit(solution)/shard_map/pallas_call | solution.py:297
  13.6 0.6 %copy.7 = f32[1,8,5,512]{3,1,2,0:T(8,128)} copy(f32[1,8,5,512]{3,1,2,0:T(8,128)S(1)} %bitcast.11) | data formatting | bytes 163840

commit v3 on v2

--- a/solution.py
+++ b/solution.py
@@ -12,7 +12,8 @@
 LANES = 128
 GAMMA = 1.4
 COURANT = 0.8
-OFFSETS = (-2, -1, 1, 2)
+REACH = 2
+OFFSETS = (-2, 2, -1, 1)
 
 
 def prims(cells):
@@ -36,22 +37,22 @@
     return parts, jnp.abs(normal) + sound
 
 
-def kernel(ranges, slabs, slots, message, state_hbm, count_hbm, near_hbm, send_hbm, ghost_hbm, out_ref,
+def kernel(ranges, slabs, phases, slots, message, state_hbm, count_hbm, near_hbm, send_hbm, ghost_hbm, out_ref,
            state, count, near, send, ghost, faces, rolled, outbox, inbox, vertical, above, below,
-           ghosts, top_out, top_in, slab_out, slab_in,
+           ghosts, top_out, top_in,
            load_sem, table_sem, face_send, face_recv, vert_send, vert_recv,
-           top_send, top_recv, slab_send, slab_recv):
+           top_send, top_recv):
     me = lax.axis_index("morton")
     slab = lax.axis_index("group")
     tiles = state.shape[2] // LANES
 
     barrier = pltpu.get_barrier_semaphore()
-    for step in range(1, slabs):
-        pl.semaphore_signal(barrier, inc=1, device_id={"group": lax.rem(slab + step, slabs)},
-                            device_id_type=pl.DeviceIdType.MESH)
-    for step in range(1, ranges):
-        pl.semaphore_signal(barrier, inc=1, device_id={"morton": lax.rem(me + step, ranges)},
-                            device_id_type=pl.DeviceIdType.MESH)
+    def device(step):
+        return {"group": lax.rem(slab + step[0], slabs), "morton": lax.rem(me + step[1], ranges)}
+
+    for phase in phases:
+        for step in phase:
+            pl.semaphore_signal(barrier, inc=1, device_id=device(step), device_id_type=pl.DeviceIdType.MESH)
 
     loads = [
         pltpu.make_async_copy(state_hbm, state, load_sem)
@@ -61,7 +62,7 @@
         for i, (source, target) in enumerate(
             ((count_hbm, count), (near_hbm, near), (send_hbm, send), (ghost_hbm, ghost)))
     ]
-    for copy in loads + tables:
+    for copy in tables + loads:
         copy.start()
 
     lane = lax.broadcasted_iota(jnp.int32, (slots, LANES), 1)
@@ -87,49 +88,9 @@
         bound = jnp.where(valid, bound, 0.0)
         top = bound if top is None else jnp.maximum(top, bound)
     top = jnp.max(top, axis=0, keepdims=True)
-    top_out[...] = top
-
-    take_y = lane // 8 % 2 * 64 + lane // 64 * 56 + lane % 8
-    take_z = lane // 8 % 2 * 64 + lane % 8 * 8 + lane // 64 * 7
-    piece = lane % 64 // 16
-
-    def compact(v, index):
-        found = permuted(cells[0][v], index)
-        for c in range(1, tiles):
-            found = jnp.where(piece == c, permuted(cells[c][v], index), found)
-        return found
-
-    own = [
-        [jnp.where(low_half, cells[0][v], cells[tiles - 1][v]) for v in range(VARS)],
-        [compact(v, take_y) for v in range(VARS)],
-        [compact(v, take_z) for v in range(VARS)],
-    ]
-    face_rows = faces.reshape(2 * slots * 8, LANES)
-    rolled_rows = rolled.reshape(2 * slots * 8, LANES)
-    zero = jnp.zeros((slots, LANES), jnp.float32)
-    for p in range(2):
-        for v in range(8):
-            value = own[p][v] if v < VARS else zero
-            face_rows[pl.ds(p * slots * 8 + v, slots, stride=8), :] = value
-            rolled_rows[pl.ds(p * slots * 8 + v, slots, stride=8), :] = (
-                pltpu.roll(value, 64, 1) if v < VARS else zero)
-    for v in range(VARS):
-        vertical[v] = own[2][v]
-
-    tables[2].wait()
-    tile_low = lax.broadcasted_iota(jnp.int32, (8, LANES), 1) < LANES // 2
-    for o, offset in enumerate(OFFSETS):
-        target = lax.rem(me + offset + ranges, ranges)
-        for t in range(message):
-            entry = send[t, 0, target]
-            safe = jnp.maximum(entry, 0)
-            face = safe % 4
-            index = face // 2 * slots + safe // 4
-            straight, turned = faces[index], rolled[index]
-            picked = jnp.where(tile_low == (face % 2 == 0), straight, turned)
-            outbox[o, t] = jnp.where(entry >= 0, picked, 0.0)
-
-    pl.semaphore_wait(barrier, ranges - 1 + slabs - 1)
+    top_out[0] = top
+
+    pl.semaphore_wait(barrier, sum(len(phase) for phase in phases))
 
     def remote(source, target, send_at, recv_at, device):
         copy = pltpu.make_async_remote_copy(
@@ -138,20 +99,96 @@
         copy.start()
         return copy
 
-    top_copies = [
-        remote(top_out, top_in.at[step - 1], top_send.at[step - 1], top_recv.at[step - 1],
-               {"morton": lax.rem(me + step, ranges)})
-        for step in range(1, ranges)
-    ]
-    face_copies = [
-        remote(outbox.at[o], inbox.at[len(OFFSETS) - 1 - o], face_send.at[o], face_recv.at[len(OFFSETS) - 1 - o],
-               {"morton": lax.rem(me + offset + ranges, ranges)})
-        for o, offset in enumerate(OFFSETS)
-    ]
-    vert_copies = [
-        remote(vertical, below, vert_send.at[0], vert_recv.at[0], {"group": lax.rem(slab + 1, slabs)}),
-        remote(vertical, above, vert_send.at[1], vert_recv.at[1], {"group": lax.rem(slab + slabs - 1, slabs)}),
-    ]
+    def exchange(source, number):
+        first_slot = sum(len(phase) for phase in phases[:number])
+        return [
+            (remote(source, top_in.at[n], top_send.at[n], top_recv.at[n], device(step)), n)
+            for n, step in enumerate(phases[number], first_slot)
+        ]
+
+    def gathered(top, copies):
+        for copy, n in copies:
+            copy.wait_recv()
+        for copy, n in copies:
+            top = jnp.maximum(top, top_in[n])
+        return top
+
+    top_copies = exchange(top_out.at[0], 0)
+
+    take_y = lane // 8 % 2 * 64 + lane // 64 * 56 + lane % 8
+    take_z = lane // 8 % 2 * 64 + lane % 8 * 8 + lane // 64 * 7
+    piece = lane % 64 // 16
+
+    def compact(v, index):
+        found = permuted(cells[0][v], index)
+        for c in range(1, tiles):
+            found = jnp.where(piece == c, permuted(cells[c][v], index), found)
+        return found
+
+    own = [
+        [jnp.where(low_half, cells[0][v], cells[tiles - 1][v]) for v in range(VARS)],
+        [compact(v, take_y) for v in range(VARS)],
+        [compact(v, take_z) for v in range(VARS)],
+    ]
+    face_rows = faces.reshape(2 * slots * 8, LANES)
+    rolled_rows = rolled.reshape(2 * slots * 8, LANES)
+    for p in range(2):
+        for v in range(VARS):
+            value = own[p][v]
+            face_rows[pl.ds(p * slots * 8 + v, slots, stride=8), :] = value
+            rolled_rows[pl.ds(p * slots * 8 + v, slots, stride=8), :] = pltpu.roll(value, 64, 1)
+    turned = [pltpu.roll(value, 64, 1) for value in own[2]]
+    for v in range(0, VARS, 2):
+        last_one = v + 1 == VARS
+        vertical[0, v // 2] = turned[v] if last_one else jnp.where(low_half, turned[v], own[2][v + 1])
+        vertical[1, v // 2] = own[2][v] if last_one else jnp.where(low_half, own[2][v], turned[v + 1])
+
+    tables[2].wait()
+    tile_low = lax.broadcasted_iota(jnp.int32, (8, LANES), 1) < LANES // 2
+    for o, offset in enumerate(OFFSETS):
+        target = jnp.clip(me + offset, 0, ranges - 1)
+        for t in range(message):
+            entry = send[t, 0, target]
+            safe = jnp.maximum(entry, 0)
+            face = safe & 3
+            index = (face >> 1) * slots + (safe >> 2)
+            straight, turned = faces[index], rolled[index]
+            picked = jnp.where(tile_low == ((face & 1) == 0), straight, turned)
+            outbox[o, t] = jnp.where(entry >= 0, picked, 0.0)
+
+    def guarded(source, target, send_at, recv_at, device, sends, receives):
+        copy = pltpu.make_async_remote_copy(
+            src_ref=source, dst_ref=target, send_sem=send_at, recv_sem=recv_at,
+            device_id=device, device_id_type=pl.DeviceIdType.MESH)
+        pl.when(sends)(copy.start)
+        return copy, sends, receives
+
+    edge_copies = [
+        guarded(vertical.at[0], below, vert_send.at[0], vert_recv.at[0],
+                {"group": jnp.minimum(slab + 1, slabs - 1)}, slab < slabs - 1, slab > 0),
+        guarded(vertical.at[1], above, vert_send.at[1], vert_recv.at[1],
+                {"group": jnp.maximum(slab - 1, 0)}, slab > 0, slab < slabs - 1),
+    ]
+    for o, offset in enumerate(OFFSETS):
+        sends = (me + offset >= 0) & (me + offset < ranges)
+        receives = (me - offset >= 0) & (me - offset < ranges)
+        edge_copies.append(guarded(
+            outbox.at[o, :, pl.ds(0, VARS), :],
+            inbox.at[pl.ds((REACH - offset) * message, message), pl.ds(0, VARS), :],
+            face_send.at[o], face_recv.at[o],
+            {"morton": jnp.clip(me + offset, 0, ranges - 1)}, sends, receives))
+
+    tables[1].wait()
+    tables[3].wait()
+    for s in range(slots):
+        for p in range(2):
+            halves = []
+            for k in (2 * p, 2 * p + 1):
+                local = near[0, k, s] - me * slots
+                inside = (local >= 0) & (local < slots)
+                local = jnp.clip(local, 0, slots - 1)
+                halves.append(jnp.where(inside, rolled[p * slots + local], faces[p * slots + s]))
+            ghosts[p * slots + s] = jnp.where(tile_low, halves[0], halves[1])
 
     def shift_up(values, axis):
         if axis == 0:
@@ -203,48 +240,41 @@
 
     own_flux = [flux_along(own[axis], prims(own[axis]), axis) for axis in range(3)]
 
-    for copy in top_copies:
-        copy.wait_recv()
-    top = top_out[...]
-    for step in range(1, ranges):
-        top = jnp.maximum(top, top_in[step - 1])
-    slab_out[...] = top
-    slab_copies = [
-        remote(slab_out, slab_in.at[step - 1], slab_send.at[step - 1], slab_recv.at[step - 1],
-               {"group": lax.rem(slab + step, slabs)})
-        for step in range(1, slabs)
-    ]
-
-    tables[1].wait()
-    tables[3].wait()
-    for copy in face_copies + vert_copies:
-        copy.wait_recv()
+    if len(phases) > 1:
+        top = gathered(top_out[0], top_copies)
+        top_out[1] = top
+        slab_copies = exchange(top_out.at[1], 1)
+    else:
+        top, slab_copies = top_out[0], []
+
+    for copy, sends, receives in edge_copies:
+        pl.when(receives)(copy.wait_recv)
     for s in range(slots):
         for p in range(2):
             halves = []
             for k in (2 * p, 2 * p + 1):
                 arrives = ghost[0, k, s]
-                neighbour = near[0, k, s]
-                inside = (neighbour >= 0) & (neighbour // slots == me)
-                local = jnp.where(inside, neighbour % slots, s)
-                here = jnp.where(inside, rolled[p * slots + local], faces[p * slots + s])
-                safe = jnp.maximum(arrives, 0)
-                distance = safe // message - me
-                box = jnp.where(distance < 0, distance + 2, distance + 1)
-                box = jnp.clip(box, 0, len(OFFSETS) - 1)
-                there = inbox[box, safe % message]
-                halves.append(jnp.where(arrives >= 0, there, here))
-            ghosts[p * slots + s] = jnp.where(tile_low, halves[0], halves[1])
+                place = jnp.clip(arrives - (me - REACH) * message, 0, (2 * REACH + 1) * message - 1)
+                half = tile_low if k % 2 == 0 else ~tile_low
+                halves.append((half & (arrives >= 0), inbox[place]))
+            value = ghosts[p * slots + s]
+            for mask, there in halves:
+                value = jnp.where(mask, there, value)
+            ghosts[p * slots + s] = value
     ghost_rows = ghosts.reshape(2 * slots * 8, LANES)
     outer = [
         [ghost_rows[pl.ds(p * slots * 8 + v, slots, stride=8), :] for v in range(VARS)]
         for p in range(2)
     ]
     use_own = jnp.where(low_half, (slab == 0).astype(jnp.int32), (slab == slabs - 1).astype(jnp.int32)) > 0
-    outer.append([
-        jnp.where(use_own, own[2][v], pltpu.roll(jnp.where(low_half, above[v], below[v]), 64, 1))
-        for v in range(VARS)
-    ])
+    outer.append([])
+    for v in range(VARS):
+        low, high = below[v // 2], above[v // 2]
+        if v % 2 == 0:
+            high = pltpu.roll(high, 64, 1)
+        else:
+            low = pltpu.roll(low, 64, 1)
+        outer[2].append(jnp.where(use_own, own[2][v], jnp.where(low_half, low, high)))
     sign = jnp.where(low_half, -1.0, 1.0)
     for axis in range(3):
         outer_flux, outer_speed = flux_along(outer[axis], prims(outer[axis]), axis)
@@ -267,21 +297,26 @@
                     edge = first[axis][c] | last[axis][c]
                     change[c][v] = change[c][v] + jnp.where(edge, permuted(signed, index), 0.0)
 
-    for copy in slab_copies:
-        copy.wait_recv()
-    for step in range(1, slabs):
-        top = jnp.maximum(top, slab_in[step - 1])
+    top = gathered(top, slab_copies or top_copies)
     step_size = COURANT / jnp.max(top, axis=1, keepdims=True)
     for c in range(tiles):
         for v in range(VARS):
             value = jnp.where(valid, cells[c][v] - step_size * change[c][v], 0.0)
             out_ref[v, :, pl.ds(c * LANES, LANES)] = value
-    for copy in top_copies + face_copies + vert_copies + slab_copies:
+    for copy, n in top_copies + slab_copies:
         copy.wait_send()
+    for copy, sends, receives in edge_copies:
+        pl.when(sends)(copy.wait_send)
 
 
 def solution(mesh):
     ranges, slabs = mesh.shape["morton"], mesh.shape["group"]
+
+    along_group = [(g, 0) for g in range(1, slabs)]
+    along_morton = [(0, r) for r in range(1, ranges)]
+    across = [(g, r) for g in range(1, slabs) for r in range(1, ranges)]
+    phases = [across + along_group + along_morton] if ranges * slabs <= 64 else [along_morton, along_group]
+    partners = sum(len(phase) for phase in phases)
 
     def per_device(state, patch_count, neighbour_table, send_table, ghost_table):
         _, slots, variables, count_cells = state.shape
@@ -295,7 +330,7 @@
         send_table = jnp.transpose(send_table, (2, 0, 1))
         ghost_table = jnp.transpose(ghost_table, (0, 2, 1))
         out = pl.pallas_call(
-            functools.partial(kernel, ranges, slabs, slots, message),
+            functools.partial(kernel, ranges, slabs, phases, slots, message),
             out_shape=pltpu.VMEM(state.shape, f32),
             in_specs=[pl.BlockSpec(memory_space=pltpu.HBM)] * 5,
             out_specs=pl.BlockSpec(memory_space=pltpu.VMEM),
@@ -308,25 +343,21 @@
                 vmem((2 * slots, 8, LANES), f32),
                 vmem((2 * slots, 8, LANES), f32),
                 vmem((len(OFFSETS), message, 8, LANES), f32),
-                vmem((len(OFFSETS), message, 8, LANES), f32),
-                vmem((VARS, slots, LANES), f32),
-                vmem((VARS, slots, LANES), f32),
-                vmem((VARS, slots, LANES), f32),
+                vmem(((2 * REACH + 1) * message, 8, LANES), f32),
+                vmem((2, (VARS + 1) // 2, slots, LANES), f32),
+                vmem(((VARS + 1) // 2, slots, LANES), f32),
+                vmem(((VARS + 1) // 2, slots, LANES), f32),
                 vmem((2 * slots, 8, LANES), f32),
-                vmem((1, LANES), f32),
-                vmem((ranges - 1, 1, LANES), f32),
-                vmem((1, LANES), f32),
-                vmem((slabs - 1, 1, LANES), f32),
+                vmem((2, 1, LANES), f32),
+                vmem((partners, 1, LANES), f32),
                 dma,
                 dma((4,)),
                 dma((len(OFFSETS),)),
                 dma((len(OFFSETS),)),
                 dma((2,)),
                 dma((2,)),
-                dma((ranges - 1,)),
-                dma((ranges - 1,)),
-                dma((slabs - 1,)),
-                dma((slabs - 1,)),
+                dma((partners,)),
+                dma((partners,)),
             ],
             compiler_params=pltpu.CompilerParams(collective_id=0, has_side_effects=True),
         )(state, patch_count, neighbour_table, send_table, ghost_table)

time: 14.4 us -> 12.3 us (0.85)
  Pallas kernels: 12.9 us -> 10.9 us
    pallas_call x1, Pallas kernels: 12.9 us -> 10.9 us  [per_device(): pl.pallas_call(functools.partial(kernel, ranges, slabs, phases, slots, me...]
where the time goes in v3:
time: 12.3 us; the launch traced here: 12.2 us
  Pallas kernels  10.9 us (89%)
  between operations  0.66 us (5%)
  local copies, waits for them, and re-layouts  0.64 us (5%)
    pallas_call x1, Pallas kernels, per_device(): pl.pallas_call(functools.partial(kernel, ranges, slabs, phases, slots, me...  10.9 us
    unnamed x1, local copies, waits for them, and re-layouts  0.64 us

profile of v3, /device:TPU:0, one launch (start us, length us, event | category | flops | bytes accessed | tf_op | source)
XLA Modules:
  0.0 12.2 jit_solution(8846958415280338185)
XLA Ops:
  0.7 10.9 %shard_map.55 = f32[5,8,512]{2,1,0:T(8,128)S(1)} custom-call(f32[5,8,512]{2,1,0:T(8,128)} %bitcast.12, s32[1,1]{1,0:T(1,128)} %bitcast.10.count_hbm, s32[1,4,8]{2,1,0:T(4,128)} %bitcast.14, s32[5,1,8]{2,1,0:T(1,128)} %bitcast.13, s32[1,4,8]{2,1,0:T(4,128)} %bitcast.15), custom_call_target="tpu_custom_call" | custom-call | tf_op jit(solution)/shard_map/pallas_call | solution.py:332
  11.5 0.6 %copy.7 = f32[1,8,5,512]{3,1,2,0:T(8,128)} copy(f32[1,8,5,512]{3,1,2,0:T(8,128)S(1)} %bitcast.11) | data formatting | bytes 163840

commit v4 on v3

--- a/solution.py
+++ b/solution.py
@@ -37,6 +37,15 @@
     return parts, jnp.abs(normal) + sound
 
 
+def flipped(index, bits):
+    bit = 1
+    while bit <= bits:
+        if bits & bit:
+            index = index + bit * (1 - 2 * (index // bit % 2))
+        bit *= 2
+    return index
+
+
 def kernel(ranges, slabs, phases, slots, message, state_hbm, count_hbm, near_hbm, send_hbm, ghost_hbm, out_ref,
            state, count, near, send, ghost, faces, rolled, outbox, inbox, vertical, above, below,
            ghosts, top_out, top_in,
@@ -48,7 +57,9 @@
 
     barrier = pltpu.get_barrier_semaphore()
     def device(step):
-        return {"group": lax.rem(slab + step[0], slabs), "morton": lax.rem(me + step[1], ranges)}
+        if slabs & (slabs - 1) or ranges & (ranges - 1):
+            return {"group": lax.rem(slab + step[0], slabs), "morton": lax.rem(me + step[1], ranges)}
+        return {"group": flipped(slab, step[0]), "morton": flipped(me, step[1])}
 
     for phase in phases:
         for step in phase:
@@ -312,9 +323,9 @@
 def solution(mesh):
     ranges, slabs = mesh.shape["morton"], mesh.shape["group"]
 
-    along_group = [(g, 0) for g in range(1, slabs)]
-    along_morton = [(0, r) for r in range(1, ranges)]
-    across = [(g, r) for g in range(1, slabs) for r in range(1, ranges)]
+    along_group = [(g, 0) for g in range(slabs - 1, 0, -1)]
+    along_morton = [(0, r) for r in range(ranges - 1, 0, -1)]
+    across = [(g, r) for g in range(slabs - 1, 0, -1) for r in range(ranges - 1, 0, -1)]
     phases = [across + along_group + along_morton] if ranges * slabs <= 64 else [along_morton, along_group]
     partners = sum(len(phase) for phase in phases)
 

time: 12.3 us -> 12.4 us (level)
  no operation moved by 1% of the time
where the time goes in v4:
time: 12.4 us; the launch traced here: 12.2 us
  Pallas kernels  10.9 us (88%)
  between operations  0.66 us (5%)
  local copies, waits for them, and re-layouts  0.64 us (5%)
    pallas_call x1, Pallas kernels, per_device(): pl.pallas_call(functools.partial(kernel, ranges, slabs, phases, slots, me...  10.9 us
    unnamed x1, local copies, waits for them, and re-layouts  0.64 us

profile of v4, /device:TPU:0, one launch (start us, length us, event | category | flops | bytes accessed | tf_op | source)
XLA Modules:
  0.0 12.2 jit_solution(4221303799389560386)
XLA Ops:
  0.7 10.9 %shard_map.55 = f32[5,8,512]{2,1,0:T(8,128)S(1)} custom-call(f32[5,8,512]{2,1,0:T(8,128)} %bitcast.12, s32[1,1]{1,0:T(1,128)} %bitcast.10.count_hbm, s32[1,4,8]{2,1,0:T(4,128)} %bitcast.14, s32[5,1,8]{2,1,0:T(1,128)} %bitcast.13, s32[1,4,8]{2,1,0:T(4,128)} %bitcast.15), custom_call_target="tpu_custom_call" | custom-call | tf_op jit(solution)/shard_map/pallas_call | solution.py:343
  11.6 0.6 %copy.7 = f32[1,8,5,512]{3,1,2,0:T(8,128)} copy(f32[1,8,5,512]{3,1,2,0:T(8,128)S(1)} %bitcast.11) | data formatting | bytes 163840
